TPU v7x, 32 devices: a whole 2x2x4 slice. The times are simulated.
32 devices in a mesh: band: 4 (over z), px: 4 (over x, core), py: 2 (over y).
Axes of the slice: x: 2, y: 2, z: 4, core: 2. Of those that a mesh axis runs over, the one named last changes fastest.
Arguments:
- orbitals: bfloat16 [4, 1024, 384], P('band', ('px', 'py')), may hold values from -0.01171875 to 0.01171875
- occupations: float32 [4], P('band'), may hold values from 0.2 to 2
- stick_map: int32 [2, 1024], P(None, 'px'), may hold values from 0 to 191, as said below
- core_density: float32 [192, 192, 192], P('py', 'px'), may hold values from 0.05 to 0.5
Outputs:
- potential: float32 [192, 192, 192], P('py', 'px')
- gradient: float32 [3, 192, 192, 192], P(None, 'py', 'px')
Inputs may be any that keep to these rules, and one draw needn't show every extreme that they name: `stick_map`: columns i * 128 * 2 to (i + 1) * 128 * 2 - 1 have x index from i * 48 to (i + 1) * 48 - 1; no two columns share a grid position.
All inputs are finite; a program needn't handle non-finite values.
Results may differ from a plain program's by a relative error of at most 0.0054.
Values may be sent and summed in bfloat16 or wider, within the bound.
No kernel may reach another device: no remote copies, remote signals or barrier semaphores. Data moves between devices by JAX's collectives and lax.ppermute only.
A program may use at most 128 MiB of HBM per device.

v0:
```python
import math
import jax
import jax.numpy as jnp
from jax import lax
from jax.sharding import PartitionSpec as P

SPACING = 0.25
PBE_KAPPA = 0.804
PBE_MU = 0.2195
SLATER_COEF = 0.75 * (3.0 / math.pi) ** (1.0 / 3.0)
REDUCED_SCALE = 4.0 * (3.0 * math.pi**2) ** (2.0 / 3.0)
HIGHEST_PREC = lax.Precision.HIGHEST


def complex_table(row_index, col_index, points, direction):
    product = row_index[:, None] * col_index[None, :] % points
    angles = 2.0 * math.pi / points * product.astype(jnp.float32)
    cosine = jnp.cos(angles)
    sine_part = direction * jnp.sin(angles)
    return jnp.stack([jnp.stack([cosine, sine_part], 1), jnp.stack([-sine_part, cosine], 1)], 0)


def freq_pair(positions, points):
    signed = jnp.where(positions <= points // 2, positions, positions - points).astype(jnp.float32)
    gradient_freq = jnp.where(positions == points // 2, 0.0, signed)
    return (signed, gradient_freq)


def swap_rows(values):
    return lax.all_to_all(values, "px", split_axis=1, concat_axis=0, tiled=True)


def swap_depth(values):
    moved = lax.all_to_all(values, ("band", "py"), split_axis=1, concat_axis=0, tiled=True)
    return moved


def exchange_part(density, fields):
    cube_root = jnp.cbrt(density)
    four_thirds = density * cube_root
    grad_square = fields[1] * fields[1] + fields[2] * fields[2] + fields[3] * fields[3]
    reduced = grad_square / (REDUCED_SCALE * four_thirds * four_thirds)
    denominator = 1.0 + PBE_MU * reduced / PBE_KAPPA
    enhance = 1.0 + PBE_KAPPA - PBE_KAPPA / denominator
    enhance_slope = PBE_MU / (denominator * denominator)
    potential = fields[0] - SLATER_COEF * cube_root * (
        4.0 / 3.0 * enhance - 8.0 / 3.0 * reduced * enhance_slope
    )
    return jnp.concatenate([potential[None], fields[1:]], 0)


def transform(rho_local, pieces, depth_index, px_index):
    zshare, y_rows, points = rho_local.shape
    rows_px = lax.axis_size("px")
    rows_py = lax.axis_size("py")
    xblock = points // rows_px
    kyblock = points // pieces
    zblock = zshare * (pieces // rows_py)
    every_index = jnp.arange(points, dtype=jnp.int32)
    forward = complex_table(every_index, every_index, points, -1.0)
    x_table = forward[0].reshape(points, 2, rows_px, xblock).transpose(0, 2, 1, 3)
    section_data = jnp.einsum("zyx,xbsk->ybzsk", rho_local, x_table, precision=HIGHEST_PREC)
    section_data = swap_rows(section_data.reshape(y_rows, rows_px, zshare * 2 * xblock))
    section_data = section_data.reshape(points, zshare, 2, xblock)
    y_table = forward.reshape(2, points, 2, pieces, kyblock)
    section_data = jnp.einsum("yzrx,rysdk->zdksx", section_data, y_table, precision=HIGHEST_PREC)
    section_data = swap_depth(section_data.reshape(zshare, pieces, kyblock * 2 * xblock))
    section_data = section_data.reshape(pieces * zshare, kyblock, 2, xblock)
    source = jnp.arange(pieces * zshare, dtype=jnp.int32)
    device = source // zshare
    within = source % zshare
    z_order = device % rows_py * zblock + device // rows_py * zshare + within
    z_table = complex_table(z_order, every_index, points, -1.0)
    spectrum = jnp.einsum("zyrx,rzsk->kysx", section_data, z_table, precision=HIGHEST_PREC)
    q_depth, g_depth = freq_pair(every_index, points)
    ky_index = depth_index * kyblock + jnp.arange(kyblock, dtype=jnp.int32)
    q_col, g_col = freq_pair(ky_index, points)
    kx_index = px_index * xblock + jnp.arange(xblock, dtype=jnp.int32)
    q_row, g_row = freq_pair(kx_index, points)
    wave_unit = 2.0 * math.pi / (points * SPACING)
    squared = wave_unit**2 * (
        q_depth[:, None, None] ** 2 + q_col[None, :, None] ** 2 + q_row[None, None, :] ** 2
    )
    hartree = jnp.where(squared > 0, 4.0 * math.pi / jnp.where(squared > 0, squared, 1.0), 0.0)
    wave_z = wave_unit * g_depth[:, None, None]
    wave_y = wave_unit * g_col[None, :, None]
    wave_x = wave_unit * g_row[None, None, :]
    real_part = spectrum[:, :, 0, :]
    imag_part = spectrum[:, :, 1, :]
    first_factor = hartree - wave_x
    packed = jnp.stack(
        [
            jnp.stack([first_factor * real_part, first_factor * imag_part], 2),
            jnp.stack(
                [-wave_z * real_part - wave_y * imag_part, wave_y * real_part - wave_z * imag_part],
                2,
            ),
        ],
        0,
    )
    inverse = complex_table(every_index, every_index, points, 1.0)
    zi_table = complex_table(every_index, z_order, points, 1.0).reshape(
        2, points, 2, pieces, zshare
    )
    section_data = jnp.einsum("fkyrx,rksdz->ydfzsx", packed, zi_table, precision=HIGHEST_PREC)
    section_data = swap_depth(section_data.reshape(kyblock, pieces, 2 * zshare * 2 * xblock))
    section_data = section_data.reshape(points, 2, zshare, 2, xblock)
    yi_table = inverse.reshape(2, points, 2, rows_px, y_rows)
    section_data = jnp.einsum("kfzrx,rksby->xbfzsy", section_data, yi_table, precision=HIGHEST_PREC)
    section_data = swap_rows(section_data.reshape(xblock, rows_px, 2 * zshare * 2 * y_rows))
    section_data = section_data.reshape(points, 2, zshare, 2, y_rows)
    fields = jnp.einsum("kfzry,rksx->fszyx", section_data, inverse, precision=HIGHEST_PREC)
    fields = fields * (1.0 / float(points) ** 3)
    return fields.reshape(4, zshare, y_rows, points)


def body(orbitals, occupations, stick_map, core_density):
    bands_here, columns_here, doubled = orbitals.shape
    points = doubled // 2
    rows_px = lax.axis_size("px")
    rows_py = lax.axis_size("py")
    groups = lax.axis_size("band")
    px_index = lax.axis_index("px")
    py_index = lax.axis_index("py")
    xblock = points // rows_px
    zblock = points // rows_py
    y_rows = points // rows_px
    every_index = jnp.arange(points, dtype=jnp.int32)
    inverse = complex_table(every_index, every_index, points, 1.0)
    z_table = (
        inverse.reshape(2, points, 2, rows_py, zblock)
        .transpose(0, 1, 3, 2, 4)
        .reshape(doubled, doubled)
    )
    columns = jnp.dot(
        orbitals.astype(jnp.float32).reshape(bands_here * columns_here, doubled),
        z_table,
        precision=HIGHEST_PREC,
    )
    columns = columns.astype(jnp.bfloat16).reshape(bands_here, columns_here, doubled)
    columns = lax.all_to_all(columns, "py", split_axis=2, concat_axis=1, tiled=True)
    slot_index = stick_map[1] * xblock + (stick_map[0] - px_index * xblock)
    plane_data = (
        jnp.zeros((bands_here, points * xblock, 2 * zblock), jnp.float32)
        .at[:, slot_index]
        .set(columns.astype(jnp.float32))
    )
    plane_data = plane_data.reshape(bands_here, points, xblock, 2, zblock)
    plane_data = jnp.einsum("byxrz,rysk->bkxsz", plane_data, inverse, precision=HIGHEST_PREC)
    plane_data = plane_data.astype(jnp.bfloat16).reshape(bands_here, points, xblock * 2 * zblock)
    plane_data = lax.all_to_all(plane_data, "px", split_axis=1, concat_axis=2, tiled=True)
    plane_data = plane_data.astype(jnp.float32).reshape(bands_here, y_rows, points, 2, zblock)
    orbital_values = jnp.einsum("byxrz,rxsk->bszyk", plane_data, inverse, precision=HIGHEST_PREC)
    density = jnp.einsum(
        "b,bszyk->zyk", occupations, orbital_values * orbital_values, precision=HIGHEST_PREC
    )
    zshare = zblock // groups
    band_index = lax.axis_index("band")
    shared_rows = lax.psum_scatter(density, "band", scatter_dimension=0, tiled=True)
    core_rows = lax.dynamic_slice_in_dim(core_density, band_index * zshare, zshare, 0)
    rho_local = shared_rows + core_rows
    fields = transform(rho_local, groups * rows_py, band_index * rows_py + py_index, px_index)
    results = lax.all_gather(exchange_part(rho_local, fields), "band", axis=1, tiled=True)
    return (results[0], results[1:4])


def solution(mesh):
    return jax.shard_map(
        body,
        mesh=mesh,
        in_specs=(P("band", ("px", "py"), None), P("band"), P(None, "px"), P("py", "px", None)),
        out_specs=(P("py", "px", None), P(None, "py", "px", None)),
        check_vma=False,
    )
```

profile of v0, /device:TPU:0, one launch (start us, length us, event | category | flops | bytes accessed | tf_op | source)
XLA Modules:
  0.0 1160.9 jit_solution(13728535052132577211)
XLA Ops:
  7.2 0.8 fusion.90
  10.8 1.2 reduce.3
  12.6 4.3 all-to-all-start
  16.9 0.8 fusion.121
  17.7 0.8 fusion.111
  18.6 2.7 all-to-all-done
  21.9 5.9 scatter_custom_fusion
  27.8 12.3 %reshape.807 = f32[192,48,2,96]{3,2,1,0:T(2,128)} reshape(f32[9216,192]{1,0:T(8,128)} %scatter_custom_fusion) | data formatting | bytes 14155776 | tf_op jit(solution)/shard_map/reshape.2
  40.1 14.2 %copy.140 = f32[192,48,2,96]{0,3,2,1:T(8,128)} copy(f32[192,48,2,96]{3,2,1,0:T(2,128)} %reshape.807) | data formatting | bytes 14155776 | tf_op jit(solution)/shard_map/reshape.2
  54.3 18.6 %fusion.5 = bf16[1,192,48,2,96]{1,4,2,3,0:T(8,128)(2,1)} fusion(f32[192,48,2,96]{0,3,2,1:T(8,128)} %copy.140, f32[1,192,2,192]{3,1,0,2:T(8,128)S(1)} %get-tuple-element.11, f32[1,192,2,192]{3,1,0,2:T(8,128)S(1)} %get-tuple-element.10), kind=kOutput, calls=%fused_computation.8 | convolution fusion | flops 8155643904 | bytes 11206656 | tf_op jit(solution)/shard_map/byxrz,rysk->bkxsz/dot_general | solution.py:149
  72.8 11.6 copy.141
  84.4 24.4 %reshape.857 = bf16[1,192,9216]{2,0,1:T(2,128)(2,1)} reshape(bf16[1,192,48,2,96]{4,3,2,1,0:T(2,128)(2,1)} %copy.141) | data formatting | bytes 7077888 | tf_op jit(solution)/shard_map/reshape | solution.py:150
  108.8 78.5 %reduce.4 = bf16[192,9216]{1,0:T(8,128)(2,1)} reduce(bf16[192,1,9216]{2,1,0:T(2,128)(2,1)} %bitcast.221, bf16[]{:T(256)} %broadcast.1309), dimensions={1}, to_apply=%bitcast.207.reduce_sub_computation | reduce | bytes 7077890
  187.3 5.6 reshape.864
  192.9 4.7 all-to-all-start.1
  198.3 40.5 %all-to-all-done.1 = bf16[4,2,221184]{2,1,0:T(2,128)(2,1)} async-done(((bf16[4,2,221184]{2,1,0:T(2,128)(2,1)}), bf16[4,2,221184]{2,1,0:T(2,128)(2,1)}, u32[]{:S(2)}, u32[]{:S(2)}) %all-to-all-start.1) | async-done | bytes 3538976 | tf_op jit(solution)/shard_map/all_to_all | solution.py:151
  238.8 6.6 reshape.865
  245.4 4.1 copy.194
  249.5 4.5 copy.143
  254.0 14.9 %reshape.809 = bf16[48,192,2,96]{3,2,1,0:T(2,128)(2,1)} reshape(bf16[1,48,4,9216]{3,2,1,0:T(4,128)(2,1)} %copy.143) | data formatting | bytes 7077888 | tf_op jit(solution)/shard_map/reshape.5
  268.9 10.5 fusion.2
  279.5 2.5 multiply_bitcast_fusion
  282.0 6.8 copy.146
  288.8 0.9 fusion.94
  289.7 84.4 %reduce-scatter.2.cloned.1.call-done = f32[24,48,192]{2,1,0:T(8,128)} async-done(((f32[96,48,192]{2,1,0:T(8,128)}), f32[24,48,192]{2,1,0:T(8,128)}) %reduce-scatter.2.cloned.1.call-update) | async-done | bytes 884752 | tf_op jit(solution)/shard_map/reduce_scatter | solution.py:159
  374.1 6.7 convolution_bitcast_fusion
  380.9 7.5 copy.147
  388.4 9.3 reshape.811
  397.7 3.8 all-to-all-start.2
  401.5 0.9 sine_multiply_fusion.1
  402.4 21.2 %all-to-all-done.2 = f32[48,4,2304]{2,0,1:T(8,128)S(1)} async-done(((f32[48,4,2304]{2,0,1:T(8,128)}), f32[48,4,2304]{2,0,1:T(8,128)S(1)}, u32[]{:S(2)}, u32[]{:S(2)}) %all-to-all-start.2) | async-done | bytes 1769504 | tf_op jit(solution)/shard_map/all_to_all | solution.py:30
  423.6 8.6 reshape.812
  432.2 10.4 fusion.27
  442.6 5.8 copy.186
  448.4 9.7 reshape.858
  458.1 5.1 all-to-all-start.3
  463.3 0.9 sine_multiply_fusion.2
  464.2 0.9 maximum_bitcast_fusion.14
  465.2 1.6 fusion.103
  466.9 37.3 %all-to-all-done.3 = f32[24,8,2304]{2,0,1:T(8,128)S(1)} async-done(((f32[24,8,2304]{2,0,1:T(8,128)}), f32[24,8,2304]{2,0,1:T(8,128)S(1)}, u32[]{:S(2)}, u32[]{:S(2)}) %all-to-all-start.3) | async-done | bytes 1769504 | tf_op jit(solution)/shard_map/all_to_all | solution.py:34
  504.1 8.6 reshape.814
  512.7 5.7 copy.152
  518.4 5.1 fusion.34
  523.6 0.8 slice_multiply_fusion.4
  525.6 15.9 %fusion.22 = f32[24,8,2,24,2,48]{5,3,0,2,1,4:T(8,128)S(1)} fusion(f32[1,192,24,2,48]{1,4,2,3,0:T(8,128)S(1)} %maximum_bitcast_fusion.5, f32[1,192,24,2,48]{1,4,2,3,0:T(8,128)S(1)} %maximum_bitcast_fusion.4, f32[1,192,1,8,24]{1,4,0,3,2:T(8,128)S(1)} %copy-done.4, f32[1,192,1,8,24]{1,4,0,3,2:T(8,128)S(1)} %copy-done.3, ...), kind=kOutput, calls=%fused_computation.28 | convolution fusion | flops 4078190592 | bytes 7520256 | tf_op jit(solution)/shard_map/fkyrx,rksdz->ydfzsx/dot_general | solution.py:105
  541.5 8.0 copy.189
  549.5 16.6 %reshape.859 = f32[24,8,4608]{2,0,1:T(8,128)} reshape(f32[24,8,2,24,2,48]{5,4,3,2,0,1:T(2,128)} %copy.189) | data formatting | bytes 7077888 | tf_op jit(solution)/shard_map/reshape | solution.py:106
  566.1 4.5 all-to-all-start.4
  570.6 0.9 fusion.107
  571.5 77.6 %all-to-all-done.4 = f32[24,8,4608]{2,0,1:T(8,128)} async-done(((f32[24,8,4608]{2,0,1:T(8,128)}), f32[24,8,4608]{2,0,1:T(8,128)}, u32[]{:S(2)}, u32[]{:S(2)}) %all-to-all-start.4) | async-done | bytes 3538976 | tf_op jit(solution)/shard_map/all_to_all | solution.py:34
  649.2 17.3 %reshape.816 = f32[192,2,24,2,48]{4,3,2,1,0:T(2,128)} reshape(f32[8,24,1,4608]{3,1,0,2:T(8,128)} %bitcast.63) | data formatting | bytes 7077888 | tf_op jit(solution)/shard_map/reshape | solution.py:107
  666.5 24.9 %fusion.19 = f32[48,4,2,24,2,48]{0,5,3,2,1,4:T(8,128)} fusion(f32[192,2,24,2,48,1,1]{4,3,2,1,0,6,5:T(2,128)} %bitcast.218, f32[1,192,1,4,48]{1,4,0,3,2:T(8,128)S(1)} %get-tuple-element.20, f32[1,192,1,4,48]{1,4,0,3,2:T(8,128)S(1)} %get-tuple-element.19, f32[1,192,1,4,48]{1,4,0,3,2:T(8,128)S(1)} %get-tuple-element.18), kind=kOutput, calls=%fused_computation.27 | convolution fusion | flops 4077305856 | bytes 7520256 | tf_op jit(solution)/shard_map/kfzrx,rksby->xbfzsy/dot_general | solution.py:109
  691.4 13.7 %copy.157 = f32[48,4,2,24,2,48]{5,4,3,2,0,1:T(2,128)} copy(f32[48,4,2,24,2,48]{0,5,3,2,1,4:T(8,128)} %fusion.19) | data formatting | bytes 7077888 | tf_op jit(solution)/shard_map/kfzrx,rksby->xbfzsy/transpose | solution.py:109
  705.1 16.6 %reshape.817 = f32[48,4,4608]{2,0,1:T(8,128)} reshape(f32[48,4,2,24,2,48]{5,4,3,2,0,1:T(2,128)} %copy.157) | data formatting | bytes 7077888 | tf_op jit(solution)/shard_map/reshape | solution.py:110
  721.7 46.9 %all_to_all.84 = f32[48,4,4608]{2,0,1:T(8,128)} all-to-all(f32[48,4,4608]{2,0,1:T(8,128)} %reshape.817), channel_id=1, replica_groups=mesh['band'=4,'px'=4,'py'=2] {'px'}, dimensions={1} | all-to-all | bytes 7077888 | tf_op jit(solution)/shard_map/all_to_all | solution.py:30
  768.6 17.1 %reshape.818 = f32[192,2,24,2,48]{4,3,2,1,0:T(2,128)} reshape(f32[4,48,1,4608]{3,1,0,2:T(8,128)} %bitcast.224) | data formatting | bytes 7077888 | tf_op jit(solution)/shard_map/reshape | solution.py:111
  785.7 13.2 %copy.158 = f32[192,2,24,2,48]{0,4,3,2,1:T(8,128)} copy(f32[192,2,24,2,48]{4,3,2,1,0:T(2,128)} %reshape.818) | data formatting | bytes 7077888 | tf_op jit(solution)/shard_map/reshape | solution.py:111
  798.9 10.3 fusion.9
  809.8 1.0 copy-done.2
  810.8 3.1 fusion.41
  814.0 2.6 pad_maximum_fusion
  816.6 320.4 %all-gather.2.cloned.1.call-done = f32[4,96,48,192]{3,2,1,0:T(8,128)} async-done(((f32[4,24,48,192]{3,2,1,0:T(8,128)}), f32[4,96,48,192]{3,2,1,0:T(8,128)}) %all-gather.2.cloned.1.call-update) | async-done | bytes 14155792 | tf_op jit(solution)/shard_map/all_gather | solution.py:163
  1137.0 4.8 slice_bitcast_fusion
  1141.8 11.8 %slice.55 = f32[3,96,48,192]{3,2,1,0:T(8,128)} slice(f32[4,96,48,192]{3,2,1,0:T(8,128)} %all-gather.2.cloned.1.call-done), slice={[1:4], [0:96], [0:48], [0:192]} | slice | bytes 21233664 | tf_op jit(solution)/shard_map/slice | solution.py:164
  (42 shorter events, 6.1 us)
Async XLA Ops:
  7.2 2.2 copy-start
  8.1 10.4 copy-start.5
  12.6 8.6 all-to-all-start
  192.9 45.9 %all-to-all-start.1 = ((bf16[4,2,221184]{2,1,0:T(2,128)(2,1)}), bf16[4,2,221184]{2,1,0:T(2,128)(2,1)}, u32[]{:S(2)}, u32[]{:S(2)}) async-start(bf16[4,2,221184]{2,1,0:T(2,128)(2,1)} %reshape.864), calls=%async_computation.1 | async-start | bytes 7077888 | tf_op jit(solution)/shard_map/all_to_all | solution.py:151
  197.6 176.5 %reduce-scatter.2.cloned.1.call-start = ((), (), s32[]{:S(2)}) async-start(), calls=%async_computation.7 | async-start | bytes 5898240 | tf_op jit(solution)/shard_map/reduce_scatter | solution.py:159
  397.7 25.9 %all-to-all-start.2 = ((f32[48,4,2304]{2,0,1:T(8,128)}), f32[48,4,2304]{2,0,1:T(8,128)S(1)}, u32[]{:S(2)}, u32[]{:S(2)}) async-start(f32[48,4,2304]{2,0,1:T(8,128)} %reshape.811), calls=%async_computation.3 | async-start | bytes 3538944 | tf_op jit(solution)/shard_map/all_to_all | solution.py:30
  458.1 46.0 %all-to-all-start.3 = ((f32[24,8,2304]{2,0,1:T(8,128)}), f32[24,8,2304]{2,0,1:T(8,128)S(1)}, u32[]{:S(2)}, u32[]{:S(2)}) async-start(f32[24,8,2304]{2,0,1:T(8,128)} %reshape.858), calls=%async_computation.4 | async-start | bytes 3538944 | tf_op jit(solution)/shard_map/all_to_all | solution.py:34
  524.6 0.9 copy-start.3
  524.6 1.0 copy-start.4
  566.1 83.1 %all-to-all-start.4 = ((f32[24,8,4608]{2,0,1:T(8,128)}), f32[24,8,4608]{2,0,1:T(8,128)}, u32[]{:S(2)}, u32[]{:S(2)}) async-start(f32[24,8,4608]{2,0,1:T(8,128)} %reshape.859), calls=%async_computation.5 | async-start | bytes 7077888 | tf_op jit(solution)/shard_map/all_to_all | solution.py:34
  570.6 566.4 %all-gather.2.cloned.1.call-start = ((), (), s32[]{:S(2)}) async-start(), calls=%async_computation.8 | async-start | bytes 23592960 | tf_op jit(solution)/shard_map/all_gather | solution.py:163
  809.6 1.3 copy-start.2
  1141.8 11.8 %copy-start.1 = (bf16[1,128,384]{2,1,0:T(8,128)(2,1)S(1)}, bf16[1,128,384]{2,1,0:T(8,128)(2,1)}, u32[]{:S(2)}) copy-start(bf16[1,128,384]{2,1,0:T(8,128)(2,1)} %param.4) | copy-start | bytes 294916
Sparse Core Ops, SparseCore 0:
  288.9 85.1 reduce-scatter.1
  816.7 320.2 all-gather.1
where the time goes:
time: 1170 us; the launch traced here: 1160 us
  waiting for transfers between devices  584 us (50%)
  local copies, waits for them, and re-layouts  291 us (25%)
  matrix products  103 us (9%)
  other arithmetic  98.1 us (8%)
  blocking collectives  46.9 us (4%)
  starting transfers between devices  22.4 us (2%)
  between operations  15.5 us (1%)
    all_gather x1, waiting for transfers between devices, body(): lax.all_gather(exchange_part(rho_local, fields), 'band', axis=1, tiled=True)  320 us
    all_to_all x2, waiting for transfers between devices, swap_depth(): lax.all_to_all(values, ('band', 'py'), split_axis=1, concat_axis=0, tiled...  115 us
    reduce_scatter x1, waiting for transfers between devices, body(): lax.psum_scatter(density, 'band', scatter_dimension=0, tiled=True)  84.4 us
    unnamed x2, other arithmetic  79.7 us
    all_to_all x1, blocking collectives, swap_rows(): return lax.all_to_all(values, 'px', split_axis=1, concat_axis=0, tiled=True)  46.9 us
    another operation x3, local copies, waits for them, and re-layouts  41.4 us
    all_to_all x1, waiting for transfers between devices, body(): lax.all_to_all(plane_data, 'px', split_axis=1, concat_axis=2, tiled=True)  40.5 us
    reshape x2, local copies, waits for them, and re-layouts, transform(): section_data = section_data.reshape(points, 2, zshare, 2, y_rows)  30.3 us
  transfers between devices with their start and end apart: 7, of which 7 were waited for; matrix products, arithmetic and copies ran while one was open for 1% of the time, Pallas kernels for 0%

commit v1 on v0

--- a/solution.py
+++ b/solution.py
@@ -27,7 +27,10 @@
 
 
 def swap_rows(values):
-    return lax.all_to_all(values, "px", split_axis=1, concat_axis=0, tiled=True)
+    return jnp.concatenate(
+        lax.all_to_all(jnp.stack(jnp.split(values, lax.axis_size("px"), axis=1)), "px", 0, 0),
+        axis=0,
+    )
 
 
 def swap_depth(values):

time: 1170 us -> 1170 us (level)
    another operation x3 -> x8, local copies, waits for them, and re-layouts: 41.4 us -> 82.6 us
    reshape x3 -> x0, local copies, waits for them, and re-layouts: 38.8 us -> none  [the longest x2 30.3 us: transform(): section_data = section_data.reshape(points, 2, zshare, 2, y_rows)]
where the time goes in v1:
time: 1170 us; the launch traced here: 1160 us
  waiting for transfers between devices  584 us (50%)
  local copies, waits for them, and re-layouts  292 us (25%)
  matrix products  103 us (9%)
  other arithmetic  99.6 us (9%)
  blocking collectives  44.7 us (4%)
  starting transfers between devices  22.4 us (2%)
  between operations  15.5 us (1%)
    all_gather x1, waiting for transfers between devices, body(): lax.all_gather(exchange_part(rho_local, fields), 'band', axis=1, tiled=True)  320 us
    all_to_all x2, waiting for transfers between devices, swap_depth(): lax.all_to_all(values, ('band', 'py'), split_axis=1, concat_axis=0, tiled...  115 us
    reduce_scatter x1, waiting for transfers between devices, body(): lax.psum_scatter(density, 'band', scatter_dimension=0, tiled=True)  84.4 us
    unnamed x2, other arithmetic  79.6 us
    all_to_all x1, blocking collectives, swap_rows(): lax.all_to_all(jnp.stack(jnp.split(values, lax.axis_size('px'), axis=1)),...  44.7 us
    another operation x3, local copies, waits for them, and re-layouts  41.4 us
    all_to_all x1, waiting for transfers between devices, body(): lax.all_to_all(plane_data, 'px', split_axis=1, concat_axis=2, tiled=True)  40.5 us
    another operation x2, local copies, waits for them, and re-layouts, transform(): section_data = section_data.reshape(points, 2, zshare, 2, y_rows)  30.3 us
  transfers between devices with their start and end apart: 7, of which 7 were waited for; matrix products, arithmetic and copies ran while one was open for 1% of the time, Pallas kernels for 0%

profile of v1, /device:TPU:0, one launch (start us, length us, event | category | flops | bytes accessed | tf_op | source)
XLA Modules:
  0.0 1161.8 jit_solution(7209765380261062271)
XLA Ops:
  7.2 0.8 fusion.90
  10.8 1.1 reduce.3
  12.6 4.3 all-to-all-start
  18.5 2.7 all-to-all-done
  21.8 5.9 scatter_custom_fusion
  27.7 12.3 %reshape.799 = f32[192,48,2,96]{3,2,1,0:T(2,128)} reshape(f32[9216,192]{1,0:T(8,128)} %scatter_custom_fusion) | data formatting | bytes 14155776 | tf_op jit(solution)/shard_map/reshape.2
  40.0 14.2 %copy.146 = f32[192,48,2,96]{0,3,2,1:T(8,128)} copy(f32[192,48,2,96]{3,2,1,0:T(2,128)} %reshape.799) | data formatting | bytes 14155776 | tf_op jit(solution)/shard_map/reshape.2
  54.2 18.6 %fusion.5 = bf16[1,192,48,2,96]{1,4,2,3,0:T(8,128)(2,1)} fusion(f32[192,48,2,96]{0,3,2,1:T(8,128)} %copy.146, f32[1,192,2,192]{3,1,0,2:T(8,128)S(1)} %get-tuple-element.19, f32[1,192,2,192]{3,1,0,2:T(8,128)S(1)} %get-tuple-element.18), kind=kOutput, calls=%fused_computation.8 | convolution fusion | flops 8155643904 | bytes 11206656 | tf_op jit(solution)/shard_map/byxrz,rysk->bkxsz/dot_general | solution.py:152
  72.8 11.6 %copy.147 = bf16[1,192,48,2,96]{4,3,2,1,0:T(2,128)(2,1)} copy(bf16[1,192,48,2,96]{1,4,2,3,0:T(8,128)(2,1)} %fusion.5) | data formatting | bytes 7077888 | tf_op jit(solution)/shard_map/convert_element_type | solution.py:153
  84.4 24.4 %reshape.847 = bf16[1,192,9216]{2,0,1:T(2,128)(2,1)} reshape(bf16[1,192,48,2,96]{4,3,2,1,0:T(2,128)(2,1)} %copy.147) | data formatting | bytes 7077888 | tf_op jit(solution)/shard_map/reshape | solution.py:153
  108.8 78.5 %reduce.4 = bf16[192,9216]{1,0:T(8,128)(2,1)} reduce(bf16[192,1,9216]{2,1,0:T(2,128)(2,1)} %bitcast.231, bf16[]{:T(256)} %broadcast.1309), dimensions={1}, to_apply=%bitcast.217.reduce_sub_computation | reduce | bytes 7077890
  187.3 5.6 reshape.854
  192.8 4.7 all-to-all-start.1
  198.3 40.5 %all-to-all-done.1 = bf16[4,2,221184]{2,1,0:T(2,128)(2,1)} async-done(((bf16[4,2,221184]{2,1,0:T(2,128)(2,1)}), bf16[4,2,221184]{2,1,0:T(2,128)(2,1)}, u32[]{:S(2)}, u32[]{:S(2)}) %all-to-all-start.1) | async-done | bytes 3538976 | tf_op jit(solution)/shard_map/all_to_all | solution.py:154
  238.8 6.6 reshape.855
  245.4 4.1 copy.200
  249.5 4.5 copy.149
  254.0 14.9 %reshape.801 = bf16[48,192,2,96]{3,2,1,0:T(2,128)(2,1)} reshape(bf16[1,48,4,9216]{3,2,1,0:T(4,128)(2,1)} %copy.149) | data formatting | bytes 7077888 | tf_op jit(solution)/shard_map/reshape.5
  268.9 10.5 fusion.2
  279.4 2.5 multiply_bitcast_fusion
  281.9 6.8 copy.152
  288.8 0.9 fusion.94
  289.7 84.4 %reduce-scatter.2.cloned.1.call-done = f32[24,48,192]{2,1,0:T(8,128)} async-done(((f32[96,48,192]{2,1,0:T(8,128)}), f32[24,48,192]{2,1,0:T(8,128)}) %reduce-scatter.2.cloned.1.call-update) | async-done | bytes 884752 | tf_op jit(solution)/shard_map/reduce_scatter | solution.py:162
  374.1 6.7 convolution_bitcast_fusion
  380.8 7.5 copy.153
  388.4 8.5 reshape.803
  397.0 1.3 pad_maximum_fusion.2
  398.3 3.8 all-to-all-start.2
  402.1 0.9 sine_multiply_fusion.1
  403.0 21.2 %all-to-all-done.2 = f32[4,48,1,2304]{3,1,2,0:T(8,128)S(1)} async-done(((f32[4,48,1,2304]{3,1,2,0:T(8,128)}), f32[4,48,1,2304]{3,1,2,0:T(8,128)S(1)}, u32[]{:S(2)}, u32[]{:S(2)}) %all-to-all-start.2) | async-done | bytes 1769504 | tf_op jit(solution)/shard_map/all_to_all | solution.py:31
  424.2 8.6 reshape_reshape.6
  432.8 10.4 fusion.27
  443.2 5.8 copy.192
  449.0 9.7 reshape.848
  458.7 5.1 all-to-all-start.3
  463.9 0.9 sine_multiply_fusion.2
  464.8 1.0 maximum_bitcast_fusion.14
  465.8 1.6 fusion.103
  467.5 37.2 %all-to-all-done.3 = f32[24,8,2304]{2,0,1:T(8,128)S(1)} async-done(((f32[24,8,2304]{2,0,1:T(8,128)}), f32[24,8,2304]{2,0,1:T(8,128)S(1)}, u32[]{:S(2)}, u32[]{:S(2)}) %all-to-all-start.3) | async-done | bytes 1769504 | tf_op jit(solution)/shard_map/all_to_all | solution.py:37
  504.7 8.6 reshape.805
  513.3 5.7 copy.158
  519.0 5.1 fusion.34
  524.2 0.8 slice_multiply_fusion.4
  526.2 15.9 %fusion.22 = f32[24,8,2,24,2,48]{5,3,0,2,1,4:T(8,128)S(1)} fusion(f32[1,192,24,2,48]{1,4,2,3,0:T(8,128)S(1)} %maximum_bitcast_fusion.5, f32[1,192,24,2,48]{1,4,2,3,0:T(8,128)S(1)} %maximum_bitcast_fusion.4, f32[1,192,1,8,24]{1,4,0,3,2:T(8,128)S(1)} %copy-done.4, f32[1,192,1,8,24]{1,4,0,3,2:T(8,128)S(1)} %copy-done.3, ...), kind=kOutput, calls=%fused_computation.29 | convolution fusion | flops 4078190592 | bytes 7520256 | tf_op jit(solution)/shard_map/fkyrx,rksdz->ydfzsx/dot_general | solution.py:108
  542.1 8.0 copy.195
  550.1 16.6 %reshape.849 = f32[24,8,4608]{2,0,1:T(8,128)} reshape(f32[24,8,2,24,2,48]{5,4,3,2,0,1:T(2,128)} %copy.195) | data formatting | bytes 7077888 | tf_op jit(solution)/shard_map/reshape | solution.py:109
  566.7 4.5 all-to-all-start.4
  571.2 0.9 fusion.107
  572.1 77.6 %all-to-all-done.4 = f32[24,8,4608]{2,0,1:T(8,128)} async-done(((f32[24,8,4608]{2,0,1:T(8,128)}), f32[24,8,4608]{2,0,1:T(8,128)}, u32[]{:S(2)}, u32[]{:S(2)}) %all-to-all-start.4) | async-done | bytes 3538976 | tf_op jit(solution)/shard_map/all_to_all | solution.py:37
  649.8 17.3 %reshape.807 = f32[192,2,24,2,48]{4,3,2,1,0:T(2,128)} reshape(f32[8,24,1,4608]{3,1,0,2:T(8,128)} %bitcast.65) | data formatting | bytes 7077888 | tf_op jit(solution)/shard_map/reshape | solution.py:110
  667.1 24.9 %fusion.19 = f32[48,4,2,24,2,48]{0,5,3,2,1,4:T(8,128)} fusion(f32[192,2,24,2,48,1,1]{4,3,2,1,0,6,5:T(2,128)} %bitcast.228, f32[1,192,1,4,48]{1,4,0,3,2:T(8,128)S(1)} %get-tuple-element.28, f32[1,192,1,4,48]{1,4,0,3,2:T(8,128)S(1)} %get-tuple-element.27, f32[1,192,1,4,48]{1,4,0,3,2:T(8,128)S(1)} %get-tuple-element.26), kind=kOutput, calls=%fused_computation.28 | convolution fusion | flops 4077305856 | bytes 7520256 | tf_op jit(solution)/shard_map/kfzrx,rksby->xbfzsy/dot_general | solution.py:112
  691.9 13.7 %copy.163 = f32[48,4,2,24,2,48]{5,4,3,2,0,1:T(2,128)} copy(f32[48,4,2,24,2,48]{0,5,3,2,1,4:T(8,128)} %fusion.19) | data formatting | bytes 7077888 | tf_op jit(solution)/shard_map/kfzrx,rksby->xbfzsy/transpose | solution.py:112
  705.7 16.6 %reshape.808 = f32[48,4,4608]{2,0,1:T(8,128)} reshape(f32[48,4,2,24,2,48]{5,4,3,2,0,1:T(2,128)} %copy.163) | data formatting | bytes 7077888 | tf_op jit(solution)/shard_map/reshape | solution.py:113
  722.3 2.2 slice_bitcast_fusion.5
  724.7 44.7 %all_to_all.64 = f32[4,48,1,4608]{3,1,2,0:T(8,128)} all-to-all(f32[4,48,1,4608]{3,1,2,0:T(8,128)S(1)} %pad_maximum_fusion.1), channel_id=1, replica_groups=mesh['band'=4,'px'=4,'py'=2] {'px'}, dimensions={0} | all-to-all | bytes 7077888 | tf_op jit(solution)/shard_map/all_to_all | solution.py:31
  769.4 17.1 %reshape_reshape.7 = f32[192,2,24,2,48]{4,3,2,1,0:T(2,128)} reshape(f32[4,48,1,4608]{3,1,2,0:T(8,128)} %all_to_all.64) | data formatting | bytes 7077888 | tf_op jit(solution)/shard_map/reshape;reshape | solution.py:114
  786.5 13.2 %copy.164 = f32[192,2,24,2,48]{0,4,3,2,1:T(8,128)} copy(f32[192,2,24,2,48]{4,3,2,1,0:T(2,128)} %reshape_reshape.7) | data formatting | bytes 7077888 | tf_op jit(solution)/shard_map/reshape;reshape | solution.py:114
  799.7 10.3 fusion.9
  810.7 1.0 copy-done.2
  811.7 3.1 fusion.41
  814.8 2.6 pad_maximum_fusion
  817.4 320.4 %all-gather.2.cloned.1.call-done = f32[4,96,48,192]{3,2,1,0:T(8,128)} async-done(((f32[4,24,48,192]{3,2,1,0:T(8,128)}), f32[4,96,48,192]{3,2,1,0:T(8,128)}) %all-gather.2.cloned.1.call-update) | async-done | bytes 14155792 | tf_op jit(solution)/shard_map/all_gather | solution.py:166
  1137.8 4.8 slice_bitcast_fusion
  1142.7 11.8 %slice.55 = f32[3,96,48,192]{3,2,1,0:T(8,128)} slice(f32[4,96,48,192]{3,2,1,0:T(8,128)} %all-gather.2.cloned.1.call-done), slice={[1:4], [0:96], [0:48], [0:192]} | slice | bytes 21233664 | tf_op jit(solution)/shard_map/slice | solution.py:167
  (46 shorter events, 8.1 us)
Async XLA Ops:
  7.2 2.2 copy-start
  8.1 10.4 copy-start.5
  12.6 8.6 all-to-all-start
  192.8 45.9 %all-to-all-start.1 = ((bf16[4,2,221184]{2,1,0:T(2,128)(2,1)}), bf16[4,2,221184]{2,1,0:T(2,128)(2,1)}, u32[]{:S(2)}, u32[]{:S(2)}) async-start(bf16[4,2,221184]{2,1,0:T(2,128)(2,1)} %reshape.854), calls=%async_computation.1 | async-start | bytes 7077888 | tf_op jit(solution)/shard_map/all_to_all | solution.py:154
  197.6 176.5 %reduce-scatter.2.cloned.1.call-start = ((), (), s32[]{:S(2)}) async-start(), calls=%async_computation.7 | async-start | bytes 5898240 | tf_op jit(solution)/shard_map/reduce_scatter | solution.py:162
  398.3 25.9 %all-to-all-start.2 = ((f32[4,48,1,2304]{3,1,2,0:T(8,128)}), f32[4,48,1,2304]{3,1,2,0:T(8,128)S(1)}, u32[]{:S(2)}, u32[]{:S(2)}) async-start(f32[4,48,1,2304]{3,1,2,0:T(8,128)} %pad_maximum_fusion.2), calls=%async_computation.3 | async-start | bytes 3538944 | tf_op jit(solution)/shard_map/all_to_all | solution.py:31
  458.7 46.0 %all-to-all-start.3 = ((f32[24,8,2304]{2,0,1:T(8,128)}), f32[24,8,2304]{2,0,1:T(8,128)S(1)}, u32[]{:S(2)}, u32[]{:S(2)}) async-start(f32[24,8,2304]{2,0,1:T(8,128)} %reshape.848), calls=%async_computation.4 | async-start | bytes 3538944 | tf_op jit(solution)/shard_map/all_to_all | solution.py:37
  525.2 0.9 copy-start.3
  525.2 1.0 copy-start.4
  566.7 83.1 %all-to-all-start.4 = ((f32[24,8,4608]{2,0,1:T(8,128)}), f32[24,8,4608]{2,0,1:T(8,128)}, u32[]{:S(2)}, u32[]{:S(2)}) async-start(f32[24,8,4608]{2,0,1:T(8,128)} %reshape.849), calls=%async_computation.5 | async-start | bytes 7077888 | tf_op jit(solution)/shard_map/all_to_all | solution.py:37
  571.2 566.6 %all-gather.2.cloned.1.call-start = ((), (), s32[]{:S(2)}) async-start(), calls=%async_computation.8 | async-start | bytes 23592960 | tf_op jit(solution)/shard_map/all_gather | solution.py:166
  810.4 1.3 copy-start.2
  1142.7 11.8 %copy-start.1 = (bf16[1,128,384]{2,1,0:T(8,128)(2,1)S(1)}, bf16[1,128,384]{2,1,0:T(8,128)(2,1)}, u32[]{:S(2)}) copy-start(bf16[1,128,384]{2,1,0:T(8,128)(2,1)} %param.4) | copy-start | bytes 294916
Sparse Core Ops, SparseCore 0:
  288.9 85.1 reduce-scatter.1
  817.6 320.2 all-gather.1
